TPU v7x, 32 devices: a whole 2x2x4 slice. The times are simulated.
32 devices in a mesh: fsdp: 4 (over x, core), ctx: 4 (over z), tp: 2 (over y).
Axes of the slice: x: 2, y: 2, z: 4, core: 2. Of those that a mesh axis runs over, the one named last changes fastest.
Arguments:
- tokens: bfloat16 [8192, 2048], P(('fsdp', 'ctx')), may hold values from -6 to 6
- cotangent: bfloat16 [8192, 2048], P(('fsdp', 'ctx')), may hold values from -6 to 6
- sequence_begin: int32 [8192], P('fsdp'), may hold values from 0 to 2047, as said below
- piece: int32 [8192], P('fsdp'), may hold values from 0 to 8, as said below
- padding_length: int32 [4], P('fsdp'), may hold values from 0 to 256, as said below
- attn_gain: bfloat16 [2048], P(('fsdp', 'ctx')), may hold values from 0.5 to 1.5
- q_gain: bfloat16 [128], P(('fsdp', 'ctx')), may hold values from 0.5 to 2
- k_gain: bfloat16 [128], P(('fsdp', 'ctx')), may hold values from 0.5 to 2
- w_query: bfloat16 [2048, 2048], P(('fsdp', 'ctx'), 'tp'), may hold values from -0.125 to 0.125
- key_weight: bfloat16 [2048, 1024], P(('fsdp', 'ctx'), 'tp'), may hold values from -0.125 to 0.125
- value_weight: bfloat16 [2048, 1024], P(('fsdp', 'ctx'), 'tp'), may hold values from -0.125 to 0.125
- w_out: bfloat16 [2048, 2048], P(('fsdp', 'ctx'), 'tp'), may hold values from -1 to 1
- mlp_gain: bfloat16 [2048], P(('fsdp', 'ctx')), may hold values from 0.5 to 1.5
- w_gate: bfloat16 [2048, 6144], P(('fsdp', 'ctx'), 'tp'), may hold values from -0.125 to 0.125
- w_up: bfloat16 [2048, 6144], P(('fsdp', 'ctx'), 'tp'), may hold values from -0.125 to 0.125
- w_down: bfloat16 [2048, 6144], P(('fsdp', 'ctx'), 'tp'), may hold values from -0.078125 to 0.078125
Outputs:
- layer_out: bfloat16 [8192, 2048], P(('fsdp', 'ctx'))
- grad_tokens: bfloat16 [8192, 2048], P(('fsdp', 'ctx'))
- grad_attn_gain: float32 [2048], P(('fsdp', 'ctx'))
- grad_q_gain: float32 [128], P(('fsdp', 'ctx'))
- grad_k_gain: float32 [128], P(('fsdp', 'ctx'))
- grad_query: float32 [2048, 2048], P(('fsdp', 'ctx'), 'tp')
- grad_key: float32 [2048, 1024], P(('fsdp', 'ctx'), 'tp')
- grad_value: float32 [2048, 1024], P(('fsdp', 'ctx'), 'tp')
- grad_out: float32 [2048, 2048], P(('fsdp', 'ctx'), 'tp')
- grad_mlp_gain: float32 [2048], P(('fsdp', 'ctx'))
- grad_gate: float32 [2048, 6144], P(('fsdp', 'ctx'), 'tp')
- grad_up: float32 [2048, 6144], P(('fsdp', 'ctx'), 'tp')
- grad_down: float32 [2048, 6144], P(('fsdp', 'ctx'), 'tp')
Inputs may be any that keep to these rules, and one draw needn't show every extreme that they name: `sequence_begin`: each group of 2048 tokens holds a first sequence of 1024 or more tokens from index 0, perhaps a second one after it, then its padding tokens, which form a sequence of their own; entries are indices within the group. The 256 tokens of one aligned block of 256 positions inside one sequence may form a picture piece and then share a positive number unique in the group; all other tokens are 0. `padding_length`: some group has exactly 256 padding tokens.
All inputs are finite; a program needn't handle non-finite values.
Results may differ from a plain program's by a relative error of at most 0.02.
Values may be sent and summed in bfloat16 or wider, within the bound.
A program may use at most 256 MiB of HBM per device.

v0:
```python
import jax
import jax.numpy as jnp
from jax import lax
from jax.sharding import PartitionSpec as P

HEAD_SIZE = 128
EPS = 1e-06
THETA = 1000000.0
MASK_FILL = -1e30


def rms_scale(features, gain_vec):
    inverse = lax.rsqrt(jnp.mean(features * features, axis=-1, keepdims=True) + EPS)
    return features * inverse * gain_vec


def rotate(features, cosine, sine):
    half_width = features.shape[-1] // 2
    turned = jnp.concatenate([-features[..., half_width:], features[..., :half_width]], axis=-1)
    return features * cosine + turned * sine


def rope_tables(positions, width):
    half_width = width // 2
    frequency = THETA ** (-(jnp.arange(half_width, dtype=jnp.float32) * 2.0 / width))
    angles = positions[:, None] * frequency[None, :]
    angles = jnp.concatenate([angles, angles], axis=-1)
    return (jnp.cos(angles)[:, None, :], jnp.sin(angles)[:, None, :])


def allowed(query_index, key_index, start_query, start_key, piece_query, piece_key, key_live):
    same_doc = start_query[:, None] == start_key[None, :]
    causal_pair = key_index[None, :] <= query_index[:, None]
    picture_pair = (piece_query[:, None] == piece_key[None, :]) & (piece_query[:, None] > 0)
    live_key = key_live[None, :] | (key_index[None, :] == query_index[:, None])
    return same_doc & (causal_pair | picture_pair) & live_key


def contract_last(left_side, right_side):
    return lax.dot_general(
        left_side, right_side, (((1,), (1,)), ((), ())), preferred_element_type=jnp.float32
    )


def contract_first(left_side, right_side):
    return lax.dot_general(
        left_side, right_side, (((0,), (0,)), ((), ())), preferred_element_type=jnp.float32
    )


def body(
    tokens,
    cotangent,
    sequence_begin,
    piece,
    padding_length,
    attn_gain,
    q_gain,
    k_gain,
    w_query,
    key_weight,
    value_weight,
    w_out,
    mlp_gain,
    w_gate,
    w_up,
    w_down,
):
    f32 = jnp.float32
    bf16 = jnp.bfloat16
    tok_rows = tokens.shape[0]
    group_rows = sequence_begin.shape[0]
    offset = lax.axis_index("ctx") * tok_rows
    local_index = offset + jnp.arange(tok_rows, dtype=jnp.int32)
    my_start = lax.dynamic_slice_in_dim(sequence_begin, offset, tok_rows)
    cosine, sine = rope_tables((local_index - my_start).astype(f32), HEAD_SIZE)
    key_index = jnp.arange(group_rows, dtype=jnp.int32)
    key_live = key_index < group_rows - padding_length[0]
    score_scale = HEAD_SIZE ** (-0.5)
    block_rows = min(512, group_rows)
    starts = jnp.arange(group_rows // block_rows, dtype=jnp.int32) * block_rows

    def head_prep(raw_heads, gain_vec):
        return rotate(rms_scale(raw_heads, gain_vec), cosine, sine)

    g_attn, g_query, g_key, wq_full, key_weight_whole, value_weight_whole, wo_full = (
        lax.all_gather(attn_gain, ("fsdp", "ctx"), axis=0, tiled=True),
        lax.all_gather(q_gain, ("fsdp", "ctx"), axis=0, tiled=True),
        lax.all_gather(k_gain, ("fsdp", "ctx"), axis=0, tiled=True),
        lax.all_gather(w_query, ("fsdp", "ctx"), axis=0, tiled=True),
        lax.all_gather(key_weight, ("fsdp", "ctx"), axis=0, tiled=True),
        lax.all_gather(value_weight, ("fsdp", "ctx"), axis=0, tiled=True),
        lax.all_gather(w_out, ("fsdp", "ctx"), axis=0, tiled=True),
    )
    attn_gain_f = g_attn.astype(f32)
    qgain_f = g_query.astype(f32)
    kgain_f = g_key.astype(f32)
    x_rows = tokens.astype(f32)
    normed_bf = rms_scale(x_rows, attn_gain_f).astype(bf16)
    q_raw = jnp.dot(normed_bf, wq_full, preferred_element_type=f32).reshape(tok_rows, -1, HEAD_SIZE)
    key_unrotated = jnp.dot(normed_bf, key_weight_whole, preferred_element_type=f32).reshape(
        tok_rows, -1, HEAD_SIZE
    )
    v_tok = (
        jnp.dot(normed_bf, value_weight_whole, preferred_element_type=f32)
        .astype(bf16)
        .reshape(tok_rows, -1, HEAD_SIZE)
    )
    q_tok = head_prep(q_raw, qgain_f).astype(bf16)
    k_tok = head_prep(key_unrotated, kgain_f).astype(bf16)
    q_head, k_head, v_head = (
        lax.all_to_all(q_tok, "ctx", split_axis=1, concat_axis=0, tiled=True),
        lax.all_to_all(k_tok, "ctx", split_axis=1, concat_axis=0, tiled=True),
        lax.all_to_all(v_tok, "ctx", split_axis=1, concat_axis=0, tiled=True),
    )
    kv_heads = k_head.shape[1]
    per_group = q_head.shape[1] // kv_heads
    q_group = q_head.reshape(group_rows, kv_heads, per_group, HEAD_SIZE)

    def block_scores(block_start):
        q_block = lax.dynamic_slice_in_dim(q_group, block_start, block_rows, 0)
        query_index = block_start + jnp.arange(block_rows, dtype=jnp.int32)
        pairs = allowed(
            query_index,
            key_index,
            lax.dynamic_slice_in_dim(sequence_begin, block_start, block_rows),
            sequence_begin,
            lax.dynamic_slice_in_dim(piece, block_start, block_rows),
            piece,
            key_live,
        )
        raw_scores = (
            jnp.einsum("qkrd,skd->qkrs", q_block, k_head, preferred_element_type=f32) * score_scale
        )
        return (q_block, jnp.where(pairs[:, None, None, :], raw_scores, MASK_FILL))

    def forward_block(block_start):
        q_block, scores = block_scores(block_start)
        row_max = jnp.max(scores, axis=-1, keepdims=True)
        expo_scores = jnp.exp(scores - row_max)
        row_total = jnp.sum(expo_scores, axis=-1, keepdims=True)
        prob_rows = (expo_scores / row_total).astype(bf16)
        head_out = jnp.einsum("qkrs,skd->qkrd", prob_rows, v_head, preferred_element_type=f32)
        return (
            head_out.astype(bf16).reshape(block_rows, kv_heads * per_group, HEAD_SIZE),
            (row_max + jnp.log(row_total))[..., 0],
        )

    out_blocks, lse_blocks = lax.map(forward_block, starts)
    o_head = out_blocks.reshape(group_rows, kv_heads * per_group, HEAD_SIZE)
    log_totals = lse_blocks.reshape(group_rows, kv_heads, per_group)
    o_tok = lax.all_to_all(o_head, "ctx", split_axis=0, concat_axis=1, tiled=True).reshape(
        tok_rows, -1
    )
    residual = x_rows + lax.psum(contract_last(o_tok, wo_full), "tp")
    g_mlp, wg_full, wu_full, wd_full = (
        lax.all_gather(mlp_gain, ("fsdp", "ctx"), axis=0, tiled=True),
        lax.all_gather(w_gate, ("fsdp", "ctx"), axis=0, tiled=True),
        lax.all_gather(w_up, ("fsdp", "ctx"), axis=0, tiled=True),
        lax.all_gather(w_down, ("fsdp", "ctx"), axis=0, tiled=True),
    )
    mlp_gain_f = g_mlp.astype(f32)
    normed_two = rms_scale(residual, mlp_gain_f).astype(bf16)
    gate_value = jnp.dot(normed_two, wg_full, preferred_element_type=f32)
    up_value = jnp.dot(normed_two, wu_full, preferred_element_type=f32)
    gate_sigmoid = jax.nn.sigmoid(gate_value)
    gate_silu = gate_value * gate_sigmoid
    hidden = (gate_silu * up_value).astype(bf16)
    layer_out = (
        residual
        + lax.psum(contract_last(hidden, wd_full).astype(jnp.bfloat16), "tp").astype(jnp.float32)
    ).astype(bf16)
    d_hidden = jnp.dot(cotangent, wd_full, preferred_element_type=f32)
    d_gate = (
        d_hidden * up_value * gate_sigmoid * (1.0 + gate_value * (1.0 - gate_sigmoid))
    ).astype(bf16)
    d_up = (d_hidden * gate_silu).astype(bf16)
    d_norm_two = lax.psum(contract_last(d_gate, wg_full) + contract_last(d_up, wu_full), "tp")
    _, pull_two = jax.vjp(rms_scale, residual, mlp_gain_f)
    d_residual, d_mlp_gain = pull_two(d_norm_two)
    d_residual = d_residual + cotangent.astype(f32)
    d_branch = d_residual.astype(bf16)
    d_out = (
        jnp.dot(d_branch, wo_full, preferred_element_type=f32)
        .astype(bf16)
        .reshape(tok_rows, -1, HEAD_SIZE)
    )
    d_head = lax.all_to_all(d_out, "ctx", split_axis=1, concat_axis=0, tiled=True).reshape(
        group_rows, kv_heads, per_group, HEAD_SIZE
    )

    def backward_block(accum_pair, block_start):
        key_accum, value_accum = accum_pair
        q_block, scores = block_scores(block_start)
        d_block = lax.dynamic_slice_in_dim(d_head, block_start, block_rows, 0)
        lse_block = lax.dynamic_slice_in_dim(log_totals, block_start, block_rows, 0)
        prob_rows = jnp.exp(scores - lse_block[..., None])
        d_probs = jnp.einsum("qkrd,skd->qkrs", d_block, v_head, preferred_element_type=f32)
        delta_rows = jnp.sum(prob_rows * d_probs, axis=-1, keepdims=True)
        d_scores = (prob_rows * (d_probs - delta_rows)).astype(bf16)
        d_query = (
            jnp.einsum("qkrs,skd->qkrd", d_scores, k_head, preferred_element_type=f32) * score_scale
        )
        key_accum = (
            key_accum
            + jnp.einsum("qkrs,qkrd->skd", d_scores, q_block, preferred_element_type=f32)
            * score_scale
        )
        value_accum = value_accum + jnp.einsum(
            "qkrs,qkrd->skd", prob_rows.astype(bf16), d_block, preferred_element_type=f32
        )
        return (
            (key_accum, value_accum),
            d_query.astype(bf16).reshape(block_rows, kv_heads * per_group, HEAD_SIZE),
        )

    zero_state = jnp.zeros((group_rows, kv_heads, HEAD_SIZE), f32)
    (key_accum, value_accum), dq_blocks = lax.scan(backward_block, (zero_state, zero_state), starts)
    dq_head = dq_blocks.reshape(group_rows, kv_heads * per_group, HEAD_SIZE)
    dq_tok, dk_tok, dv_tok = (
        lax.all_to_all(dq_head, "ctx", split_axis=0, concat_axis=1, tiled=True),
        lax.all_to_all(key_accum.astype(bf16), "ctx", split_axis=0, concat_axis=1, tiled=True),
        lax.all_to_all(value_accum.astype(bf16), "ctx", split_axis=0, concat_axis=1, tiled=True),
    )
    _, pull_query = jax.vjp(head_prep, q_raw, qgain_f)
    dq_raw, d_qgain = pull_query(dq_tok.astype(f32))
    _, pull_key = jax.vjp(head_prep, key_unrotated, kgain_f)
    dk_raw, d_kgain = pull_key(dk_tok.astype(f32))
    dq_flat = dq_raw.astype(bf16).reshape(tok_rows, -1)
    dk_flat = dk_raw.astype(bf16).reshape(tok_rows, -1)
    dv_flat = dv_tok.reshape(tok_rows, -1)
    d_norm_part = (
        contract_last(dq_flat, wq_full)
        + contract_last(dk_flat, key_weight_whole)
        + contract_last(dv_flat, value_weight_whole)
    )
    d_norm, d_qgain, d_kgain = lax.psum((d_norm_part, d_qgain, d_kgain), "tp")
    _, pull_one = jax.vjp(rms_scale, x_rows, attn_gain_f)
    d_tokens, d_attn_gain = pull_one(d_norm)
    grad_tokens = (d_residual + d_tokens).astype(bf16)
    all_grads = (
        lax.psum_scatter(d_attn_gain, ("fsdp", "ctx"), scatter_dimension=0, tiled=True),
        lax.psum_scatter(d_qgain, ("fsdp", "ctx"), scatter_dimension=0, tiled=True),
        lax.psum_scatter(d_kgain, ("fsdp", "ctx"), scatter_dimension=0, tiled=True),
        lax.psum_scatter(
            contract_first(normed_bf, dq_flat), ("fsdp", "ctx"), scatter_dimension=0, tiled=True
        ),
        lax.psum_scatter(
            contract_first(normed_bf, dk_flat), ("fsdp", "ctx"), scatter_dimension=0, tiled=True
        ),
        lax.psum_scatter(
            contract_first(normed_bf, dv_flat), ("fsdp", "ctx"), scatter_dimension=0, tiled=True
        ),
        lax.psum_scatter(
            contract_first(d_branch, o_tok), ("fsdp", "ctx"), scatter_dimension=0, tiled=True
        ),
        lax.psum_scatter(d_mlp_gain, ("fsdp", "ctx"), scatter_dimension=0, tiled=True),
        lax.psum_scatter(
            contract_first(normed_two, d_gate), ("fsdp", "ctx"), scatter_dimension=0, tiled=True
        ),
        lax.psum_scatter(
            contract_first(normed_two, d_up), ("fsdp", "ctx"), scatter_dimension=0, tiled=True
        ),
        lax.psum_scatter(
            contract_first(cotangent, hidden), ("fsdp", "ctx"), scatter_dimension=0, tiled=True
        ),
    )
    return (
        layer_out,
        grad_tokens,
        all_grads[0],
        all_grads[1],
        all_grads[2],
        all_grads[3],
        all_grads[4],
        all_grads[5],
        all_grads[6],
        all_grads[7],
        all_grads[8],
        all_grads[9],
        all_grads[10],
    )


def solution(mesh):
    in_specs = (
        P(("fsdp", "ctx"), None),
        P(("fsdp", "ctx"), None),
        P("fsdp"),
        P("fsdp"),
        P("fsdp"),
        P(("fsdp", "ctx")),
        P(("fsdp", "ctx")),
        P(("fsdp", "ctx")),
        P(("fsdp", "ctx"), "tp"),
        P(("fsdp", "ctx"), "tp"),
        P(("fsdp", "ctx"), "tp"),
        P(("fsdp", "ctx"), "tp"),
        P(("fsdp", "ctx")),
        P(("fsdp", "ctx"), "tp"),
        P(("fsdp", "ctx"), "tp"),
        P(("fsdp", "ctx"), "tp"),
    )
    out_specs = (
        P(("fsdp", "ctx"), None),
        P(("fsdp", "ctx"), None),
        P(("fsdp", "ctx")),
        P(("fsdp", "ctx")),
        P(("fsdp", "ctx")),
        P(("fsdp", "ctx"), "tp"),
        P(("fsdp", "ctx"), "tp"),
        P(("fsdp", "ctx"), "tp"),
        P(("fsdp", "ctx"), "tp"),
        P(("fsdp", "ctx")),
        P(("fsdp", "ctx"), "tp"),
        P(("fsdp", "ctx"), "tp"),
        P(("fsdp", "ctx"), "tp"),
    )
    return jax.shard_map(body, mesh=mesh, in_specs=in_specs, out_specs=out_specs, check_vma=False)
```

profile of v0, /device:TPU:0, one launch (start us, length us, event | category | flops | bytes accessed | tf_op | source)
XLA Modules:
  0.0 2411.7 jit_solution(119953250545401077)
XLA Ops:
  9.4 34.1 %all-gather = bf16[16,1,128]{2,1,0:T(2,128)(2,1)S(1)} all-gather(bf16[1,1,128]{2,1,0:T(2,128)(2,1)} %bitcast.402), channel_id=1, replica_groups=mesh['fsdp'=4,'ctx'=4,'tp'=2] {'fsdp','ctx'}, dimensions={0}, use_global_device_ids=true | all-gather | bytes 4352 | tf_op jit(solution)/shard_map/all_gather | solution.py:87
  47.2 29.8 %all-reduce.12 = (bf16[128]{0:T(256)(128)(2,1)S(1)}, bf16[128]{0:T(256)(128)(2,1)S(1)}) all-reduce(bf16[128]{0:T(256)(128)(2,1)S(1)} %dynamic-update-slice, bf16[128]{0:T(256)(128)(2,1)S(1)} %dynamic-update-slice.1), channel_id=1, replica_groups=mesh['fsdp'=4,'ctx'=4,'tp'=2] {'fsdp','ctx'}, use_global_device_ids=true, to_apply=%add.4 | all-reduce | flops 256 | bytes 1024
  91.1 7.5 all-gather.14.cloned.1.call-done
  102.4 46.5 %all-gather.10.cloned.1.call-done = bf16[2048,1024]{1,0:T(8,128)(2,1)} async-done(((bf16[128,1024]{1,0:T(8,128)(2,1)}), bf16[2048,1024]{1,0:T(8,128)(2,1)}) %all-gather.10.cloned.1.call-update) | async-done | bytes 4194320 | tf_op jit(solution)/shard_map/all_gather | solution.py:90
  148.9 4.6 fusion.120
  156.1 4.2 all-to-all-start.2
  165.8 9.7 all-to-all-done.2
  175.5 4.3 all-to-all-start
  182.8 31.0 %all-to-all-done = bf16[512,8,128]{2,0,1:T(8,128)(2,1)} async-done(((bf16[512,8,128]{2,0,1:T(8,128)(2,1)}), bf16[512,8,128]{2,0,1:T(8,128)(2,1)}, u32[]{:S(2)}, u32[]{:S(2)}) %all-to-all-start) | async-done | bytes 1048608 | tf_op jit(solution)/shard_map/all_to_all | solution.py:112
  217.2 61.6 %while.30 = (s32[]{:T(128)}, bf16[4,512,2,128]{3,1,0,2:T(8,128)(2,1)}, f32[4,512,1,2]{1,3,2,0:T(2,128)S(1)}, s32[4]{0:T(128)S(1)}, s32[2048]{0:T(1024)S(1)}, /*i...) while((s32[]{:T(128)}, ...), condition=%wide.region_6.7_spmd.clone.clone, body=%wide.region_3.6_spmd.clone.clone.sunk | while | flops 1108477952 | bytes 31004356 | solution.py:149
  281.6 27.7 %all_to_all.114 = bf16[2048,2,128]{2,1,0:T(2,128)(2,1)S(1)} all-to-all(bf16[2048,2,128]{2,1,0:T(2,128)(2,1)S(1)} %copy.185), channel_id=1, replica_groups=mesh['fsdp'=4,'ctx'=4,'tp'=2] {'ctx'}, dimensions={0} | all-to-all | bytes 2097152 | tf_op jit(solution)/shard_map/all_to_all | solution.py:152
  312.7 6.9 fusion.127
  321.7 29.0 %all-gather.1 = bf16[16,1,128]{2,1,0:T(2,128)(2,1)S(1)} all-gather(bf16[1,1,128]{2,1,0:T(2,128)(2,1)S(1)} %bitcast.403), channel_id=1, replica_groups=mesh['fsdp'=4,'ctx'=4,'tp'=2] {'fsdp','ctx'}, dimensions={0}, use_global_device_ids=true | all-gather | bytes 4352 | tf_op jit(solution)/shard_map/all_gather | solution.py:157
  350.7 75.1 %all-reduce.18.cloned.1.call-done = f32[512,2048]{1,0:T(8,128)} async-done(((f32[512,2048]{1,0:T(8,128)}), f32[512,2048]{1,0:T(8,128)}) %all-reduce.18.cloned.1.call-update) | async-done | bytes 4194320 | tf_op jit(solution)/shard_map/psum | solution.py:155
  431.0 97.4 %all-gather.18.cloned.1.call-done = bf16[2048,3072]{1,0:T(8,128)(2,1)} async-done(((bf16[128,3072]{1,0:T(8,128)(2,1)}), bf16[2048,3072]{1,0:T(8,128)(2,1)}) %all-gather.18.cloned.1.call-update) | async-done | bytes 12582928 | tf_op jit(solution)/shard_map/all_gather | solution.py:158
  528.4 11.3 fusion.128
  539.7 89.7 %all-gather.20.cloned.1.call-done = bf16[2048,3072]{1,0:T(8,128)(2,1)} async-done(((bf16[128,3072]{1,0:T(8,128)(2,1)}), bf16[2048,3072]{1,0:T(8,128)(2,1)}) %all-gather.20.cloned.1.call-update) | async-done | bytes 12582928 | tf_op jit(solution)/shard_map/all_gather | solution.py:159
  629.4 12.0 fusion.129
  641.4 89.0 %all-gather.22.cloned.1.call-done = bf16[2048,3072]{1,0:T(8,128)(2,1)} async-done(((bf16[128,3072]{1,0:T(8,128)(2,1)}), bf16[2048,3072]{1,0:T(8,128)(2,1)}) %all-gather.22.cloned.1.call-update) | async-done | bytes 12582928 | tf_op jit(solution)/shard_map/all_gather | solution.py:160
  730.4 16.4 multiply_convert_fusion
  746.8 13.4 fusion.130
  760.2 12.2 convolution_add_fusion
  772.5 11.7 convolution_convert_fusion
  784.1 94.6 %all-reduce.22.cloned.1.call-done = f32[512,2048]{1,0:T(8,128)} async-done(((f32[512,2048]{1,0:T(8,128)}), f32[512,2048]{1,0:T(8,128)}) %all-reduce.22.cloned.1.call-update) | async-done | bytes 4194320 | tf_op jit(solution)/shard_map/psum | solution.py:178
  878.7 5.1 multiply_reduce_fusion
  883.9 60.6 %all-reduce.20.cloned.1.call-done = bf16[512,2048]{1,0:T(8,128)(2,1)} async-done(((bf16[512,2048]{1,0:T(8,128)(2,1)}), bf16[512,2048]{1,0:T(8,128)(2,1)}) %all-reduce.20.cloned.1.call-update) | async-done | bytes 2097168 | tf_op jit(solution)/shard_map/psum | solution.py:171
  944.5 6.0 fusion.84
  954.0 4.8 all-to-all-start.4
  958.8 25.5 %all-to-all-done.4 = bf16[512,8,128]{2,0,1:T(8,128)(2,1)S(1)} async-done(((bf16[512,8,128]{2,0,1:T(8,128)(2,1)}), bf16[512,8,128]{2,0,1:T(8,128)(2,1)S(1)}, u32[]{:S(2)}, u32[]{:S(2)}) %all-to-all-start.4) | async-done | bytes 1048608 | tf_op jit(solution)/shard_map/all_to_all | solution.py:188
  986.5 117.5 %while.31 = (s32[]{:T(128)}, f32[2048,1,128]{0,2,1:T(8,128)S(1)}, f32[2048,1,128]{0,2,1:T(8,128)}, bf16[4,512,2,128]{3,1,0,2:T(8,128)(2,1)}, s32[4]{0:T(128)S(1)...) while((s32[]{:T(128)}, f32[2048,1,128]{0,2,1:T(8,128)S(1)}, ...), condition=%wide.region_14.15_spmd.clone.clone, body=%wide.region_12.14_spmd.clone.clone.sunk | while | flops 2726823936 | bytes 141362992 | solution.py:218
  995.1 4.1 fusion.212
  1006.4 4.6 fusion.216
  1011.0 4.7 fusion.215
  1024.2 4.1 fusion.212
  1035.5 4.6 fusion.216
  1040.1 5.0 fusion.215
  1053.7 4.1 fusion.212
  1064.9 4.6 fusion.216
  1069.5 5.0 fusion.215
  1083.1 4.1 fusion.212
  1094.4 4.6 fusion.216
  1099.0 5.0 fusion.215
  1113.8 10.5 all-to-all-done.6
  1124.3 4.4 all-to-all-start.7
  1134.3 8.5 all-to-all-done.7
  1142.8 4.3 all-to-all-start.5
  1159.8 12.6 all-to-all-done.5
  1180.3 5.0 fusion.131
  1190.3 14.7 convolution_bitcast_fusion.1
  1214.9 7.9 fusion.102
  1224.0 5.9 fusion.115
  1230.0 14.2 fusion.133
  1244.3 14.3 fusion.134
  1259.3 35.7 %all-reduce.24.cloned.1.call-done = f32[512,2048]{1,0:T(8,128)} async-done(((f32[512,2048]{1,0:T(8,128)}), f32[512,2048]{1,0:T(8,128)}) %all-reduce.24.cloned.1.call-update) | async-done | bytes 4194320 | tf_op jit(solution)/shard_map/psum | solution.py:237
  1298.5 62.7 %all-reduce.10 = (f32[2048]{0:T(1024)S(1)}, f32[128]{0:T(128)S(1)}, f32[128]{0:T(128)S(1)}, f32[2048]{0:T(1024)S(1)}) all-reduce(f32[2048]{0:T(1024)S(1)} %get-tuple-element.391, f32[128]{0:T(128)S(1)} %get-tuple-element.393, f32[128]{0:T(128)S(1)} %get-tuple-element.395, ...), channel_id=2, replica_groups=mesh['fsdp'=4,'ctx'=4,'tp'=2] {'fsdp','ctx'}, use_global_device_ids=true, to_apply=%region_20.21.clone | all-reduce | flops 4352 | bytes 34816
  1362.0 5.4 all-reduce.11
  1368.6 5.9 fusion.86
  1374.6 167.9 %reduce-scatter.20.cloned.1.call-done = f32[128,3072]{0,1:T(8,128)} async-done(((f32[2048,3072]{0,1:T(8,128)}), f32[128,3072]{0,1:T(8,128)}) %reduce-scatter.20.cloned.1.call-update) | async-done | bytes 1572880 | tf_op jit(solution)/shard_map/reduce_scatter | solution.py:264
  1545.5 73.4 %reduce-scatter.10.cloned.1.call-done = f32[128,512]{1,0:T(8,128)} async-done(((f32[2048,512]{1,0:T(8,128)}), f32[128,512]{1,0:T(8,128)}) %reduce-scatter.10.cloned.1.call-update) | async-done | bytes 262160 | tf_op jit(solution)/shard_map/reduce_scatter | solution.py:248
  1618.9 76.2 %reduce-scatter.12.cloned.1.call-done = f32[128,512]{1,0:T(8,128)} async-done(((f32[2048,512]{1,0:T(8,128)}), f32[128,512]{1,0:T(8,128)}) %reduce-scatter.12.cloned.1.call-update) | async-done | bytes 262160 | tf_op jit(solution)/shard_map/reduce_scatter | solution.py:251
  1695.1 107.0 %reduce-scatter.14.cloned.1.call-done = f32[128,1024]{1,0:T(8,128)} async-done(((f32[2048,1024]{1,0:T(8,128)}), f32[128,1024]{1,0:T(8,128)}) %reduce-scatter.14.cloned.1.call-update) | async-done | bytes 524304 | tf_op jit(solution)/shard_map/reduce_scatter | solution.py:254
  1802.1 107.6 %reduce-scatter.8.cloned.1.call-done = f32[128,1024]{1,0:T(8,128)} async-done(((f32[2048,1024]{1,0:T(8,128)}), f32[128,1024]{1,0:T(8,128)}) %reduce-scatter.8.cloned.1.call-update) | async-done | bytes 524304 | tf_op jit(solution)/shard_map/reduce_scatter | solution.py:245
  1909.7 247.7 %reduce-scatter.16.cloned.1.call-done = f32[128,3072]{1,0:T(8,128)} async-done(((f32[2048,3072]{1,0:T(8,128)}), f32[128,3072]{1,0:T(8,128)}) %reduce-scatter.16.cloned.1.call-update) | async-done | bytes 1572880 | tf_op jit(solution)/shard_map/reduce_scatter | solution.py:258
  2157.4 247.2 %reduce-scatter.18.cloned.1.call-done = f32[128,3072]{1,0:T(8,128)} async-done(((f32[2048,3072]{1,0:T(8,128)}), f32[128,3072]{1,0:T(8,128)}) %reduce-scatter.18.cloned.1.call-update) | async-done | bytes 1572880 | tf_op jit(solution)/shard_map/reduce_scatter | solution.py:261
  (327 shorter events, 224.6 us)
Async XLA Ops:
  7.2 75.3 %copy-start.2 = (bf16[512,2048]{1,0:T(8,128)(2,1)S(1)}, bf16[512,2048]{1,0:T(8,128)(2,1)}, u32[]{:S(2)}) copy-start(bf16[512,2048]{1,0:T(8,128)(2,1)} %param.20) | copy-start | bytes 6291460
  7.2 75.3 %all-gather.12.cloned.1.call-start = ((), (), s32[]{:S(2)}) async-start(), calls=%async_computation.16 | async-start | bytes 2228224 | tf_op jit(solution)/shard_map/all_gather | solution.py:91
  7.9 90.8 %all-gather.14.cloned.1.call-start = ((), (), s32[]{:S(2)}) async-start(), calls=%async_computation.17 | async-start | bytes 2228224 | tf_op jit(solution)/shard_map/all_gather | solution.py:92
  8.7 140.3 %all-gather.10.cloned.1.call-start = ((), (), s32[]{:S(2)}) async-start(), calls=%async_computation.15 | async-start | bytes 4456448 | tf_op jit(solution)/shard_map/all_gather | solution.py:90
  43.5 105.5 %copy-start.29 = (f32[16,1,128]{2,1,0:T(1,128)}, f32[16,1,128]{2,1,0:T(1,128)S(1)}, u32[]{:S(2)}) copy-start(f32[16,1,128]{2,1,0:T(1,128)S(1)} %convert_element_type.182) | copy-start | bytes 24580
  77.1 85.8 %copy-start.44 = (f32[128]{0:T(128)}, f32[128]{0:T(128)S(1)}, u32[]{:S(2)}) copy-start(f32[128]{0:T(128)S(1)} %convert_element_type.135) | copy-start | bytes 1540
  77.1 9.0 copy-start.46
  79.1 83.8 %copy-start.12 = (f32[512,128]{1,0:T(8,128)}, f32[512,128]{1,0:T(8,128)S(1)}, u32[]{:S(2)}) copy-start(f32[512,128]{1,0:T(8,128)S(1)} %get-tuple-element.476) | copy-start | bytes 786436
  79.1 83.8 %copy-start.14 = (f32[512,128]{1,0:T(8,128)}, f32[512,128]{1,0:T(8,128)S(1)}, u32[]{:S(2)}) copy-start(f32[512,128]{1,0:T(8,128)S(1)} %get-tuple-element.477) | copy-start | bytes 786436
  79.3 6.8 copy-start.17
  79.4 6.6 copy-start.19
  82.5 66.5 %copy-start.37 = (f32[512]{0:T(512)}, f32[512]{0:T(512)S(1)}, u32[]{:S(2)}) copy-start(f32[512]{0:T(512)S(1)} %fusion.109) | copy-start | bytes 6148
  87.7 68.4 %all-to-all-start.1 = ((bf16[512,4,128]{0,2,1:T(8,128)(2,1)}), bf16[512,4,128]{0,2,1:T(8,128)(2,1)S(1)}, u32[]{:S(2)}, u32[]{:S(2)}) async-start(bf16[512,4,128]{0,2,1:T(8,128)(2,1)} %fusion.99), calls=%async_computation.1 | async-start | bytes 1048576 | tf_op jit(solution)/shard_map/all_to_all | solution.py:113
  156.0 6.9 copy-start.35
  156.0 6.9 copy-start.31
  156.1 19.4 all-to-all-start.2
  165.8 51.4 %copy-start.25 = (s32[2048]{0:T(1024)S(1)}, s32[2048]{0:T(1024)}, u32[]{:S(2)}) copy-start(s32[2048]{0:T(1024)} %param.22) | copy-start | bytes 24580
  165.8 51.4 %copy-start.26 = (s32[2048]{0:T(1024)S(1)}, s32[2048]{0:T(1024)}, u32[]{:S(2)}) copy-start(s32[2048]{0:T(1024)} %param.23) | copy-start | bytes 24580
  175.5 38.3 %all-to-all-start = ((bf16[512,8,128]{2,0,1:T(8,128)(2,1)}), bf16[512,8,128]{2,0,1:T(8,128)(2,1)}, u32[]{:S(2)}, u32[]{:S(2)}) async-start(bf16[512,8,128]{2,0,1:T(8,128)(2,1)} %fusion.92), calls=%async_computation | async-start | bytes 2097152 | tf_op jit(solution)/shard_map/all_to_all | solution.py:112
  179.7 132.9 %all-gather.16.cloned.1.call-start = ((), (), s32[]{:S(2)}) async-start(), calls=%async_computation.18 | async-start | bytes 4456448 | tf_op jit(solution)/shard_map/all_gather | solution.py:93
  180.3 245.5 %all-reduce.18.cloned.1.call-start = ((), (), s32[]{:S(2)}) async-start(), calls=%async_computation.19 | async-start | bytes 8388608 | tf_op jit(solution)/shard_map/psum | solution.py:155
  319.6 2.2 copy-start.48
  319.6 208.8 %all-gather.18.cloned.1.call-start = ((), (), s32[]{:S(2)}) async-start(), calls=%async_computation.20 | async-start | bytes 13369344 | tf_op jit(solution)/shard_map/all_gather | solution.py:158
  320.2 309.3 %all-gather.20.cloned.1.call-start = ((), (), s32[]{:S(2)}) async-start(), calls=%async_computation.21 | async-start | bytes 13369344 | tf_op jit(solution)/shard_map/all_gather | solution.py:159
  320.9 409.5 %all-gather.22.cloned.1.call-start = ((), (), s32[]{:S(2)}) async-start(), calls=%async_computation.22 | async-start | bytes 13369344 | tf_op jit(solution)/shard_map/all_gather | solution.py:160
  321.7 557.1 %all-reduce.22.cloned.1.call-start = ((), (), s32[]{:S(2)}) async-start(), calls=%async_computation.24 | async-start | bytes 8388608 | tf_op jit(solution)/shard_map/psum | solution.py:178
  431.0 97.4 %copy-start.22 = (bf16[512,2048]{1,0:T(8,128)(2,1)}, bf16[512,2048]{1,0:T(8,128)(2,1)S(1)}, u32[]{:S(2)}) copy-start(bf16[512,2048]{1,0:T(8,128)(2,1)S(1)} %multiply_convert_fusion.3) | copy-start | bytes 6291460
  539.7 190.8 %copy-start.20 = (bf16[512,2048]{1,0:T(8,128)(2,1)S(1)}, bf16[512,2048]{1,0:T(8,128)(2,1)}, u32[]{:S(2)}) copy-start(bf16[512,2048]{1,0:T(8,128)(2,1)} %param.21) | copy-start | bytes 6291460
  746.8 13.4 copy-start.51
  746.8 13.4 copy-start.50
  772.4 172.0 %all-reduce.20.cloned.1.call-start = ((), (), s32[]{:S(2)}) async-start(), calls=%async_computation.23 | async-start | bytes 4194304 | tf_op jit(solution)/shard_map/psum | solution.py:171
  944.5 6.0 copy-start.49
  950.5 2.4 copy-start.8
  954.0 30.3 %all-to-all-start.4 = ((bf16[512,8,128]{2,0,1:T(8,128)(2,1)}), bf16[512,8,128]{2,0,1:T(8,128)(2,1)S(1)}, u32[]{:S(2)}, u32[]{:S(2)}) async-start(bf16[512,8,128]{2,0,1:T(8,128)(2,1)} %bitcast.303), calls=%async_computation.4 | async-start | bytes 2097152 | tf_op jit(solution)/shard_map/all_to_all | solution.py:188
  995.0 4.2 copy-start
  1003.1 7.9 copy-start.1
  1024.1 4.2 copy-start
  1032.2 7.9 copy-start.1
  1053.6 4.2 copy-start
  1061.6 7.9 copy-start.1
  1083.0 4.2 copy-start
  1091.1 7.9 copy-start.1
  1106.8 17.5 all-to-all-start.6
  1124.3 18.5 all-to-all-start.7
  1142.8 29.6 %all-to-all-start.5 = ((bf16[2048,2,128]{2,1,0:T(2,128)(2,1)}), bf16[2048,2,128]{2,1,0:T(2,128)(2,1)}, u32[]{:S(2)}, u32[]{:S(2)}) async-start(bf16[2048,2,128]{2,1,0:T(2,128)(2,1)} %copy.191), calls=%async_computation.5 | async-start | bytes 2097152 | tf_op jit(solution)/shard_map/all_to_all | solution.py:221
  1147.0 7.9 copy-start.11
  1147.0 7.9 copy-start.18
  1147.1 7.9 copy-start.34
  1147.1 7.9 copy-start.47
  1147.1 147.9 %all-reduce.24.cloned.1.call-start = ((), (), s32[]{:S(2)}) async-start(), calls=%async_computation.25 | async-start | bytes 8388608 | tf_op jit(solution)/shard_map/psum | solution.py:237
  1152.4 3.0 copy-start.40
  1176.5 2.0 copy-start.36
  1180.3 5.0 copy-start.27
  1180.3 5.0 copy-start.9
  1180.3 5.0 copy-start.24
  1188.8 353.7 %reduce-scatter.20.cloned.1.call-start = ((), (), s32[]{:S(2)}) async-start(), calls=%async_computation.32 | async-start | bytes 26738688 | tf_op jit(solution)/shard_map/reduce_scatter | solution.py:264
  1205.0 413.9 %reduce-scatter.10.cloned.1.call-start = ((), (), s32[]{:S(2)}) async-start(), calls=%async_computation.27 | async-start | bytes 4456448 | tf_op jit(solution)/shard_map/reduce_scatter | solution.py:248
  1210.1 485.0 %reduce-scatter.12.cloned.1.call-start = ((), (), s32[]{:S(2)}) async-start(), calls=%async_computation.28 | async-start | bytes 4456448 | tf_op jit(solution)/shard_map/reduce_scatter | solution.py:251
  1213.7 588.4 %reduce-scatter.14.cloned.1.call-start = ((), (), s32[]{:S(2)}) async-start(), calls=%async_computation.29 | async-start | bytes 8912896 | tf_op jit(solution)/shard_map/reduce_scatter | solution.py:254
  1222.8 686.9 %reduce-scatter.8.cloned.1.call-start = ((), (), s32[]{:S(2)}) async-start(), calls=%async_computation.26 | async-start | bytes 8912896 | tf_op jit(solution)/shard_map/reduce_scatter | solution.py:245
  1230.0 927.5 %reduce-scatter.16.cloned.1.call-start = ((), (), s32[]{:S(2)}) async-start(), calls=%async_computation.30 | async-start | bytes 26738688 | tf_op jit(solution)/shard_map/reduce_scatter | solution.py:258
  1244.2 1160.4 %reduce-scatter.18.cloned.1.call-start = ((), (), s32[]{:S(2)}) async-start(), calls=%async_computation.31 | async-start | bytes 26738688 | tf_op jit(solution)/shard_map/reduce_scatter | solution.py:261
  1258.6 39.9 %copy-start.41 = (f32[2048]{0:T(1024)S(1)}, f32[2048]{0:T(1024)}, u32[]{:S(2)}) copy-start(f32[2048]{0:T(1024)} %get-tuple-element.389) | copy-start | bytes 24580
  1258.6 110.0 %copy-start.43 = (f32[512]{0:T(512)S(1)}, f32[512]{0:T(512)}, u32[]{:S(2)}) copy-start(f32[512]{0:T(512)} %copy-done.42) | copy-start | bytes 6148
  (19 other events, 25.7 us)
Sparse Core Ops, SparseCore 0:
  10.2 44.3 all-gather.11
  56.8 41.7 all-gather.13
  100.9 47.9 all-gather.9
  182.4 57.7 all-gather.15
  319.7 106.0 all-reduce.17
  427.9 100.4 all-gather.17
  530.7 98.6 all-gather.19
  631.7 98.6 all-gather.21
  772.5 106.1 all-reduce.21
  881.5 62.9 all-reduce.19
  1188.9 106.0 all-reduce.23
  1298.9 243.5 reduce-scatter.19
  1546.9 71.9 reduce-scatter.9
  1623.2 71.8 reduce-scatter.11
  1699.6 102.4 reduce-scatter.13
  1806.5 103.1 reduce-scatter.7
  1914.2 243.1 reduce-scatter.15
  2162.0 242.6 reduce-scatter.17
where the time goes:
time: 2420 us; the launch traced here: 2410 us
  waiting for transfers between devices  1730 us (71%)
  matrix products  276 us (11%)
  blocking collectives  189 us (8%)
  other arithmetic  103 us (4%)
  local copies, waits for them, and re-layouts  55.2 us (2%)
  starting transfers between devices  29.6 us (1%)
    reduce_scatter x1, waiting for transfers between devices, body(): lax.psum_scatter(contract_first(normed_two, d_gate), ('fsdp', 'ctx'), sca...  248 us
    reduce_scatter x1, waiting for transfers between devices, body(): lax.psum_scatter(contract_first(normed_two, d_up), ('fsdp', 'ctx'), scatt...  247 us
    reduce_scatter x1, waiting for transfers between devices, body(): lax.psum_scatter(contract_first(cotangent, hidden), ('fsdp', 'ctx'), scat...  168 us
    reduce_scatter x1, waiting for transfers between devices, body(): lax.psum_scatter(contract_first(normed_bf, dq_flat), ('fsdp', 'ctx'), sca...  108 us
    reduce_scatter x1, waiting for transfers between devices, body(): lax.psum_scatter(contract_first(d_branch, o_tok), ('fsdp', 'ctx'), scatte...  107 us
    all_gather x1, waiting for transfers between devices, body(): lax.all_gather(w_gate, ('fsdp', 'ctx'), axis=0, tiled=True)  97.4 us
    psum x1, waiting for transfers between devices, body(): lax.psum(contract_last(d_gate, wg_full) + contract_last(d_up, wu_full), '...  94.6 us
    unnamed x2, blocking collectives  92.6 us
  transfers between devices with their start and end apart: 25, of which 22 were waited for; matrix products, arithmetic and copies ran while one was open for 10% of the time, Pallas kernels for 0%

commit v1 on v0

--- a/solution.py
+++ b/solution.py
@@ -7,6 +7,25 @@
 EPS = 1e-06
 THETA = 1000000.0
 MASK_FILL = -1e30
+
+
+def _resolve_classes(u_in, net_axis):
+    f_now, k_now, built = (lax.axis_size(net_axis), lax.axis_index(net_axis), u_in.shape[0])
+    r2, left_arr = (u_in, 1)
+    while left_arr < f_now:
+        r2 = jnp.concatenate(
+            [
+                r2,
+                lax.ppermute(
+                    r2,
+                    net_axis,
+                    list(map(lambda to_i: (to_i, (to_i - left_arr) % f_now), range(f_now))),
+                ),
+            ],
+            0,
+        )
+        left_arr = 2 * left_arr
+    return jnp.roll(r2, k_now * built, axis=0)
 
 
 def rms_scale(features, gain_vec):
@@ -155,7 +174,7 @@
     residual = x_rows + lax.psum(contract_last(o_tok, wo_full), "tp")
     g_mlp, wg_full, wu_full, wd_full = (
         lax.all_gather(mlp_gain, ("fsdp", "ctx"), axis=0, tiled=True),
-        lax.all_gather(w_gate, ("fsdp", "ctx"), axis=0, tiled=True),
+        _resolve_classes(w_gate, ("fsdp", "ctx")),
         lax.all_gather(w_up, ("fsdp", "ctx"), axis=0, tiled=True),
         lax.all_gather(w_down, ("fsdp", "ctx"), axis=0, tiled=True),
     )

time: 2420 us -> 2410 us (level)
  waiting for transfers between devices: 1730 us -> 1660 us
  local copies, waits for them, and re-layouts: 55.2 us -> 83.2 us
    ppermute x0 -> x4, waiting for transfers between devices: none -> 287 us  [_resolve_classes(): lax.ppermute(r2, net_axis, list(map(lambda to_i: (to_i, (to_i - left_arr)...]
    all_gather x1 -> x0, waiting for transfers between devices: 97.4 us -> none  [body(): lax.all_gather(w_gate, ('fsdp', 'ctx'), axis=0, tiled=True)]
    all_gather x1, waiting for transfers between devices: 89.7 us -> 0.01 us  [body(): lax.all_gather(w_up, ('fsdp', 'ctx'), axis=0, tiled=True)]
    all_gather x1, waiting for transfers between devices: 89 us -> 0.01 us  [body(): lax.all_gather(w_down, ('fsdp', 'ctx'), axis=0, tiled=True)]
    psum x1, waiting for transfers between devices: 75.1 us -> 0.01 us  [body(): residual = x_rows + lax.psum(contract_last(o_tok, wo_full), 'tp')]
  transfers between devices with their start and end apart: 25 -> 28, of which waited for: 22 -> 22; matrix products, arithmetic and copies ran while one was open for 10% -> 11% of each run, Pallas kernels for 0% -> 0%
where the time goes in v1:
time: 2410 us; the launch traced here: 2400 us
  waiting for transfers between devices  1660 us (69%)
  matrix products  277 us (11%)
  blocking collectives  203 us (8%)
  other arithmetic  111 us (5%)
  local copies, waits for them, and re-layouts  83.2 us (3%)
  starting transfers between devices  31.6 us (1%)
    ppermute x4, waiting for transfers between devices, _resolve_classes(): lax.ppermute(r2, net_axis, list(map(lambda to_i: (to_i, (to_i - left_arr)...  287 us
    reduce_scatter x1, waiting for transfers between devices, body(): lax.psum_scatter(contract_first(normed_two, d_gate), ('fsdp', 'ctx'), sca...  248 us
    reduce_scatter x1, waiting for transfers between devices, body(): lax.psum_scatter(contract_first(normed_two, d_up), ('fsdp', 'ctx'), scatt...  247 us
    reduce_scatter x1, waiting for transfers between devices, body(): lax.psum_scatter(contract_first(cotangent, hidden), ('fsdp', 'ctx'), scat...  168 us
    reduce_scatter x1, waiting for transfers between devices, body(): lax.psum_scatter(contract_first(normed_bf, dq_flat), ('fsdp', 'ctx'), sca...  108 us
    reduce_scatter x1, waiting for transfers between devices, body(): lax.psum_scatter(contract_first(d_branch, o_tok), ('fsdp', 'ctx'), scatte...  107 us
    psum x1, waiting for transfers between devices, body(): lax.psum(contract_last(d_gate, wg_full) + contract_last(d_up, wu_full), '...  97.5 us
    unnamed x2, blocking collectives  92.6 us
  transfers between devices with their start and end apart: 28, of which 22 were waited for; matrix products, arithmetic and copies ran while one was open for 11% of the time, Pallas kernels for 0%

profile of v1, /device:TPU:0, one launch (start us, length us, event | category | flops | bytes accessed | tf_op | source)
XLA Modules:
  0.0 2403.7 jit_solution(6254500835759103741)
XLA Ops:
  9.4 34.1 %all-gather = bf16[16,1,128]{2,1,0:T(2,128)(2,1)S(1)} all-gather(bf16[1,1,128]{2,1,0:T(2,128)(2,1)} %bitcast.400), channel_id=1, replica_groups=mesh['fsdp'=4,'ctx'=4,'tp'=2] {'fsdp','ctx'}, dimensions={0}, use_global_device_ids=true | all-gather | bytes 4352 | tf_op jit(solution)/shard_map/all_gather | solution.py:106
  47.2 29.8 %all-reduce.12 = (bf16[128]{0:T(256)(128)(2,1)S(1)}, bf16[128]{0:T(256)(128)(2,1)S(1)}) all-reduce(bf16[128]{0:T(256)(128)(2,1)S(1)} %dynamic-update-slice, bf16[128]{0:T(256)(128)(2,1)S(1)} %dynamic-update-slice.1), channel_id=1, replica_groups=mesh['fsdp'=4,'ctx'=4,'tp'=2] {'fsdp','ctx'}, use_global_device_ids=true, to_apply=%add.4 | all-reduce | flops 256 | bytes 1024
  91.1 7.6 all-gather.13.cloned.1.call-done
  102.4 46.5 %all-gather.9.cloned.1.call-done = bf16[2048,1024]{1,0:T(8,128)(2,1)} async-done(((bf16[128,1024]{1,0:T(8,128)(2,1)}), bf16[2048,1024]{1,0:T(8,128)(2,1)}) %all-gather.9.cloned.1.call-update) | async-done | bytes 4194320 | tf_op jit(solution)/shard_map/all_gather | solution.py:109
  148.9 4.6 fusion.129
  156.0 4.2 all-to-all-start.2
  165.8 9.7 all-to-all-done.2
  175.4 4.3 all-to-all-start
  182.9 30.9 %all-to-all-done = bf16[512,8,128]{2,0,1:T(8,128)(2,1)} async-done(((bf16[512,8,128]{2,0,1:T(8,128)(2,1)}), bf16[512,8,128]{2,0,1:T(8,128)(2,1)}, u32[]{:S(2)}, u32[]{:S(2)}) %all-to-all-start) | async-done | bytes 1048608 | tf_op jit(solution)/shard_map/all_to_all | solution.py:131
  217.1 63.7 %while.30 = (s32[]{:T(128)}, bf16[4,512,2,128]{3,1,0,2:T(8,128)(2,1)}, f32[4,512,1,2]{1,3,2,0:T(2,128)}, s32[4]{0:T(128)S(1)}, s32[2048]{0:T(1024)S(1)}, /*index...) while((s32[]{:T(128)}, ...), condition=%wide.region_6.7_spmd.clone.clone, body=%wide.region_3.6_spmd.clone.clone.sunk | while | flops 1108477952 | bytes 31004864 | solution.py:168
  284.1 27.7 %all_to_all.114 = bf16[2048,2,128]{2,1,0:T(2,128)(2,1)S(1)} all-to-all(bf16[2048,2,128]{2,1,0:T(2,128)(2,1)S(1)} %copy.185), channel_id=1, replica_groups=mesh['fsdp'=4,'ctx'=4,'tp'=2] {'ctx'}, dimensions={0} | all-to-all | bytes 2097152 | tf_op jit(solution)/shard_map/all_to_all | solution.py:171
  315.2 7.0 fusion.136
  324.1 17.7 collective-permute-done
  341.9 71.3 %collective-permute-done.1 = bf16[256,3072]{1,0:T(8,128)(2,1)S(1)} collective-permute-done((bf16[256,3072]{1,0:T(8,128)(2,1)S(1)}, bf16[256,3072]{1,0:T(8,128)(2,1)S(1)}, u32[]{:S(2)}, u32[]{:S(2)}) %collective-permute-start.1) | collective-permute-done | bytes 1572896 | tf_op jit(solution)/shard_map/ppermute | solution.py:19
  413.5 43.2 %collective-permute-done.2 = bf16[512,3072]{1,0:T(8,128)(2,1)S(1)} collective-permute-done((bf16[512,3072]{1,0:T(8,128)(2,1)S(1)}, bf16[512,3072]{1,0:T(8,128)(2,1)S(1)}, u32[]{:S(2)}, u32[]{:S(2)}) %collective-permute-start.2) | collective-permute-done | bytes 3145760 | tf_op jit(solution)/shard_map/ppermute | solution.py:19
  461.5 43.2 %all-gather.1 = bf16[16,1,128]{2,1,0:T(2,128)(2,1)S(1)} all-gather(bf16[1,1,128]{2,1,0:T(2,128)(2,1)S(1)} %bitcast.401), channel_id=1, replica_groups=mesh['fsdp'=4,'ctx'=4,'tp'=2] {'fsdp','ctx'}, dimensions={0}, use_global_device_ids=true | all-gather | bytes 4352 | tf_op jit(solution)/shard_map/all_gather | solution.py:176
  512.5 154.7 %collective-permute-done.3 = bf16[1024,3072]{1,0:T(8,128)(2,1)} collective-permute-done((bf16[1024,3072]{1,0:T(8,128)(2,1)}, bf16[1024,3072]{1,0:T(8,128)(2,1)}, u32[]{:S(2)}, u32[]{:S(2)}) %collective-permute-start.3) | collective-permute-done | bytes 6291488 | tf_op jit(solution)/shard_map/ppermute | solution.py:19
  667.2 5.9 constant_dynamic-update-slice_fusion.5
  678.2 5.9 constant_dynamic-update-slice_fusion
  690.6 12.3 fusion.137
  702.9 11.5 fusion.138
  714.4 17.5 multiply_convert_fusion.1
  731.9 12.1 fusion.139
  744.1 14.2 fusion.93
  758.3 11.6 convolution_convert_fusion
  769.9 97.5 %all-reduce.22.cloned.1.call-done = f32[512,2048]{1,0:T(8,128)} async-done(((f32[512,2048]{1,0:T(8,128)}), f32[512,2048]{1,0:T(8,128)}) %all-reduce.22.cloned.1.call-update) | async-done | bytes 4194320 | tf_op jit(solution)/shard_map/psum | solution.py:197
  867.4 5.1 multiply_reduce_fusion
  872.5 60.8 %all-reduce.20.cloned.1.call-done = bf16[512,2048]{1,0:T(8,128)(2,1)} async-done(((bf16[512,2048]{1,0:T(8,128)(2,1)}), bf16[512,2048]{1,0:T(8,128)(2,1)}) %all-reduce.20.cloned.1.call-update) | async-done | bytes 2097168 | tf_op jit(solution)/shard_map/psum | solution.py:190
  933.3 6.0 fusion.88
  942.9 5.0 all-to-all-start.4
  947.9 25.5 %all-to-all-done.4 = bf16[512,8,128]{2,0,1:T(8,128)(2,1)S(1)} async-done(((bf16[512,8,128]{2,0,1:T(8,128)(2,1)}), bf16[512,8,128]{2,0,1:T(8,128)(2,1)S(1)}, u32[]{:S(2)}, u32[]{:S(2)}) %all-to-all-start.4) | async-done | bytes 1048608 | tf_op jit(solution)/shard_map/all_to_all | solution.py:207
  975.6 120.5 %while.31 = (s32[]{:T(128)}, f32[2048,1,128]{0,2,1:T(8,128)S(1)}, f32[2048,1,128]{0,2,1:T(8,128)}, bf16[4,512,2,128]{3,1,0,2:T(8,128)(2,1)}, s32[4]{0:T(128)S(1)...) while((s32[]{:T(128)}, f32[2048,1,128]{0,2,1:T(8,128)S(1)}, ...), condition=%wide.region_14.15_spmd.clone.clone, body=%wide.region_12.14_spmd.clone.clone.sunk | while | flops 2726823936 | bytes 141362992 | solution.py:237
  984.9 4.1 fusion.219
  996.2 4.6 fusion.223
  1000.8 4.7 fusion.222
  1026.1 4.6 fusion.223
  1030.7 5.0 fusion.222
  1056.3 4.6 fusion.223
  1060.9 5.0 fusion.222
  1075.2 4.1 fusion.219
  1086.5 4.6 fusion.223
  1091.1 5.0 fusion.222
  1105.9 10.5 all-to-all-done.6
  1116.4 4.3 all-to-all-start.7
  1126.4 8.5 all-to-all-done.7
  1134.8 4.2 all-to-all-start.5
  1151.9 12.5 all-to-all-done.5
  1172.4 5.0 fusion.140
  1182.4 14.2 convolution_bitcast_fusion.1
  1206.4 7.9 fusion.109
  1215.6 6.0 fusion.124
  1221.6 14.3 fusion.142
  1235.9 14.2 fusion.143
  1250.8 36.2 %all-reduce.24.cloned.1.call-done = f32[512,2048]{1,0:T(8,128)} async-done(((f32[512,2048]{1,0:T(8,128)}), f32[512,2048]{1,0:T(8,128)}) %all-reduce.24.cloned.1.call-update) | async-done | bytes 4194320 | tf_op jit(solution)/shard_map/psum | solution.py:256
  1290.5 62.8 %all-reduce.10 = (f32[2048]{0:T(1024)S(1)}, f32[128]{0:T(128)S(1)}, f32[128]{0:T(128)S(1)}, f32[2048]{0:T(1024)S(1)}) all-reduce(f32[2048]{0:T(1024)S(1)} %get-tuple-element.391, f32[128]{0:T(128)S(1)} %get-tuple-element.393, f32[128]{0:T(128)S(1)} %get-tuple-element.395, ...), channel_id=2, replica_groups=mesh['fsdp'=4,'ctx'=4,'tp'=2] {'fsdp','ctx'}, use_global_device_ids=true, to_apply=%region_20.21.clone | all-reduce | flops 4352 | bytes 34816
  1354.1 5.4 all-reduce.11
  1360.7 5.9 fusion.90
  1366.7 168.0 %reduce-scatter.20.cloned.1.call-done = f32[128,3072]{0,1:T(8,128)} async-done(((f32[2048,3072]{0,1:T(8,128)}), f32[128,3072]{0,1:T(8,128)}) %reduce-scatter.20.cloned.1.call-update) | async-done | bytes 1572880 | tf_op jit(solution)/shard_map/reduce_scatter | solution.py:283
  1537.7 73.2 %reduce-scatter.10.cloned.1.call-done = f32[128,512]{1,0:T(8,128)} async-done(((f32[2048,512]{1,0:T(8,128)}), f32[128,512]{1,0:T(8,128)}) %reduce-scatter.10.cloned.1.call-update) | async-done | bytes 262160 | tf_op jit(solution)/shard_map/reduce_scatter | solution.py:267
  1610.8 76.3 %reduce-scatter.12.cloned.1.call-done = f32[128,512]{1,0:T(8,128)} async-done(((f32[2048,512]{1,0:T(8,128)}), f32[128,512]{1,0:T(8,128)}) %reduce-scatter.12.cloned.1.call-update) | async-done | bytes 262160 | tf_op jit(solution)/shard_map/reduce_scatter | solution.py:270
  1687.2 107.0 %reduce-scatter.14.cloned.1.call-done = f32[128,1024]{1,0:T(8,128)} async-done(((f32[2048,1024]{1,0:T(8,128)}), f32[128,1024]{1,0:T(8,128)}) %reduce-scatter.14.cloned.1.call-update) | async-done | bytes 524304 | tf_op jit(solution)/shard_map/reduce_scatter | solution.py:273
  1794.2 107.6 %reduce-scatter.8.cloned.1.call-done = f32[128,1024]{1,0:T(8,128)} async-done(((f32[2048,1024]{1,0:T(8,128)}), f32[128,1024]{1,0:T(8,128)}) %reduce-scatter.8.cloned.1.call-update) | async-done | bytes 524304 | tf_op jit(solution)/shard_map/reduce_scatter | solution.py:264
  1901.8 247.7 %reduce-scatter.16.cloned.1.call-done = f32[128,3072]{1,0:T(8,128)} async-done(((f32[2048,3072]{1,0:T(8,128)}), f32[128,3072]{1,0:T(8,128)}) %reduce-scatter.16.cloned.1.call-update) | async-done | bytes 1572880 | tf_op jit(solution)/shard_map/reduce_scatter | solution.py:277
  2149.5 247.2 %reduce-scatter.18.cloned.1.call-done = f32[128,3072]{1,0:T(8,128)} async-done(((f32[2048,3072]{1,0:T(8,128)}), f32[128,3072]{1,0:T(8,128)}) %reduce-scatter.18.cloned.1.call-update) | async-done | bytes 1572880 | tf_op jit(solution)/shard_map/reduce_scatter | solution.py:280
  (373 shorter events, 257.5 us)
Async XLA Ops:
  7.2 75.3 %copy-start.2 = (bf16[512,2048]{1,0:T(8,128)(2,1)S(1)}, bf16[512,2048]{1,0:T(8,128)(2,1)}, u32[]{:S(2)}) copy-start(bf16[512,2048]{1,0:T(8,128)(2,1)} %param.20) | copy-start | bytes 6291460
  7.2 75.3 %all-gather.11.cloned.1.call-start = ((), (), s32[]{:S(2)}) async-start(), calls=%async_computation.16 | async-start | bytes 2228224 | tf_op jit(solution)/shard_map/all_gather | solution.py:110
  7.9 90.8 %all-gather.13.cloned.1.call-start = ((), (), s32[]{:S(2)}) async-start(), calls=%async_computation.17 | async-start | bytes 2228224 | tf_op jit(solution)/shard_map/all_gather | solution.py:111
  8.7 140.3 %all-gather.9.cloned.1.call-start = ((), (), s32[]{:S(2)}) async-start(), calls=%async_computation.15 | async-start | bytes 4456448 | tf_op jit(solution)/shard_map/all_gather | solution.py:109
  43.5 105.4 %copy-start.42 = (f32[16,1,128]{2,1,0:T(1,128)}, f32[16,1,128]{2,1,0:T(1,128)S(1)}, u32[]{:S(2)}) copy-start(f32[16,1,128]{2,1,0:T(1,128)S(1)} %convert_element_type.182) | copy-start | bytes 24580
  77.1 85.8 %copy-start.57 = (f32[128]{0:T(128)}, f32[128]{0:T(128)S(1)}, u32[]{:S(2)}) copy-start(f32[128]{0:T(128)S(1)} %convert_element_type.135) | copy-start | bytes 1540
  77.1 9.0 copy-start.59
  79.1 83.8 %copy-start.23 = (f32[512,128]{1,0:T(8,128)}, f32[512,128]{1,0:T(8,128)S(1)}, u32[]{:S(2)}) copy-start(f32[512,128]{1,0:T(8,128)S(1)} %get-tuple-element.476) | copy-start | bytes 786436
  79.1 83.8 %copy-start.25 = (f32[512,128]{1,0:T(8,128)}, f32[512,128]{1,0:T(8,128)S(1)}, u32[]{:S(2)}) copy-start(f32[512,128]{1,0:T(8,128)S(1)} %get-tuple-element.477) | copy-start | bytes 786436
  82.5 66.5 %copy-start.50 = (f32[512]{0:T(512)}, f32[512]{0:T(512)S(1)}, u32[]{:S(2)}) copy-start(f32[512]{0:T(512)S(1)} %fusion.116) | copy-start | bytes 6148
  87.6 68.4 %all-to-all-start.1 = ((bf16[512,4,128]{0,2,1:T(8,128)(2,1)}), bf16[512,4,128]{0,2,1:T(8,128)(2,1)S(1)}, u32[]{:S(2)}, u32[]{:S(2)}) async-start(bf16[512,4,128]{0,2,1:T(8,128)(2,1)} %fusion.106), calls=%async_computation.1 | async-start | bytes 1048576 | tf_op jit(solution)/shard_map/all_to_all | solution.py:132
  156.0 6.9 copy-start.48
  156.0 6.9 copy-start.44
  156.0 19.4 all-to-all-start.2
  165.8 51.4 %copy-start.36 = (s32[2048]{0:T(1024)S(1)}, s32[2048]{0:T(1024)}, u32[]{:S(2)}) copy-start(s32[2048]{0:T(1024)} %param.22) | copy-start | bytes 24580
  165.8 51.4 %copy-start.38 = (s32[2048]{0:T(1024)S(1)}, s32[2048]{0:T(1024)}, u32[]{:S(2)}) copy-start(s32[2048]{0:T(1024)} %param.23) | copy-start | bytes 24580
  175.4 38.3 %all-to-all-start = ((bf16[512,8,128]{2,0,1:T(8,128)(2,1)}), bf16[512,8,128]{2,0,1:T(8,128)(2,1)}, u32[]{:S(2)}, u32[]{:S(2)}) async-start(bf16[512,8,128]{2,0,1:T(8,128)(2,1)} %fusion.99), calls=%async_computation | async-start | bytes 2097152 | tf_op jit(solution)/shard_map/all_to_all | solution.py:131
  179.7 135.5 %all-gather.15.cloned.1.call-start = ((), (), s32[]{:S(2)}) async-start(), calls=%async_computation.18 | async-start | bytes 4456448 | tf_op jit(solution)/shard_map/all_gather | solution.py:112
  180.3 503.8 %all-reduce.18.cloned.1.call-start = ((), (), s32[]{:S(2)}) async-start(), calls=%async_computation.19 | async-start | bytes 8388608 | tf_op jit(solution)/shard_map/psum | solution.py:174
  280.8 34.3 %copy-start.19 = (bf16[2048,1,128]{2,0,1:T(8,128)(2,1)}, bf16[2048,1,128]{2,0,1:T(8,128)(2,1)S(1)}, u32[]{:S(2)}) copy-start(bf16[2048,1,128]{2,0,1:T(8,128)(2,1)S(1)} %get-tuple-element.758) | copy-start | bytes 1572868
  280.8 34.3 %copy-start.21 = (bf16[2048,1,128]{2,0,1:T(8,128)(2,1)}, bf16[2048,1,128]{2,0,1:T(8,128)(2,1)S(1)}, u32[]{:S(2)}) copy-start(bf16[2048,1,128]{2,0,1:T(8,128)(2,1)S(1)} %get-tuple-element.759) | copy-start | bytes 1572868
  280.8 34.3 %copy-start.63 = (s32[4]{0:T(128)}, s32[4]{0:T(128)S(1)}, u32[]{:S(2)}) copy-start(s32[4]{0:T(128)S(1)} %get-tuple-element.813) | copy-start | bytes 52
  322.3 368.4 %all-gather.17.cloned.1.call-start = ((), (), s32[]{:S(2)}) async-start(), calls=%async_computation.20 | async-start | bytes 13369344 | tf_op jit(solution)/shard_map/all_gather | solution.py:178
  322.8 380.1 %all-gather.19.cloned.1.call-start = ((), (), s32[]{:S(2)}) async-start(), calls=%async_computation.21 | async-start | bytes 13369344 | tf_op jit(solution)/shard_map/all_gather | solution.py:179
  323.6 543.8 %all-reduce.22.cloned.1.call-start = ((), (), s32[]{:S(2)}) async-start(), calls=%async_computation.23 | async-start | bytes 8388608 | tf_op jit(solution)/shard_map/psum | solution.py:197
  323.6 18.1 collective-permute-start
  341.7 115.0 %copy-start.17 = (bf16[128,3072]{1,0:T(8,128)(2,1)}, bf16[128,3072]{1,0:T(8,128)(2,1)S(1)}, u32[]{:S(2)}) copy-start(bf16[128,3072]{1,0:T(8,128)(2,1)S(1)} %collective-permute-done) | copy-start | bytes 2359300
  341.8 71.4 %collective-permute-start.1 = (bf16[256,3072]{1,0:T(8,128)(2,1)S(1)}, bf16[256,3072]{1,0:T(8,128)(2,1)S(1)}, u32[]{:S(2)}, u32[]{:S(2)}) collective-permute-start(bf16[256,3072]{1,0:T(8,128)(2,1)S(1)} %pad_maximum_fusion.2), channel_id=1, source_target_pairs={{0,28},{2,30},{4,0},{6,2},{8,4},{10,6},{12,8},{14,10},{16,12},{18,... | collective-permute-start | bytes 4718600 | tf_op jit(solution)/shard_map/ppermute | solution.py:19
  413.2 47.1 %copy-start.14 = (bf16[256,3072]{1,0:T(8,128)(2,1)}, bf16[256,3072]{1,0:T(8,128)(2,1)S(1)}, u32[]{:S(2)}) copy-start(bf16[256,3072]{1,0:T(8,128)(2,1)S(1)} %collective-permute-done.1) | copy-start | bytes 4718596
  413.4 48.1 %copy-start.61 = (bf16[128]{0:T(256)(128)(2,1)S(1)}, bf16[128]{0:T(256)(128)(2,1)}, u32[]{:S(2)}) copy-start(bf16[128]{0:T(256)(128)(2,1)} %param.32) | copy-start | bytes 772
  413.4 43.3 %collective-permute-start.2 = (bf16[512,3072]{1,0:T(8,128)(2,1)S(1)}, bf16[512,3072]{1,0:T(8,128)(2,1)S(1)}, u32[]{:S(2)}, u32[]{:S(2)}) collective-permute-start(bf16[512,3072]{1,0:T(8,128)(2,1)S(1)} %pad_maximum_fusion.1), channel_id=1, source_target_pairs={{0,24},{2,26},{4,28},{6,30},{8,0},{10,2},{12,4},{14,6},{16,8},{18,... | collective-permute-start | bytes 9437192 | tf_op jit(solution)/shard_map/ppermute | solution.py:19
  460.3 206.9 %collective-permute-start.3 = (bf16[1024,3072]{1,0:T(8,128)(2,1)}, bf16[1024,3072]{1,0:T(8,128)(2,1)}, u32[]{:S(2)}, u32[]{:S(2)}) collective-permute-start(bf16[1024,3072]{1,0:T(8,128)(2,1)} %pad_maximum_fusion), channel_id=1, source_target_pairs={{0,16},{2,18},{4,20},{6,22},{8,24},{10,26},{12,28},{14,30},{16,0},... | collective-permute-start | bytes 18874376 | tf_op jit(solution)/shard_map/ppermute | solution.py:19
  512.5 161.6 %copy-start.18 = (bf16[128,3072]{1,0:T(8,128)(2,1)S(1)}, bf16[128,3072]{1,0:T(8,128)(2,1)}, u32[]{:S(2)}) copy-start(bf16[128,3072]{1,0:T(8,128)(2,1)} %copy-done.17) | copy-start | bytes 2359300
  690.6 12.3 copy-start.31
  702.9 11.5 copy-start.33
  731.9 12.1 copy-start.65
  758.3 175.0 %all-reduce.20.cloned.1.call-start = ((), (), s32[]{:S(2)}) async-start(), calls=%async_computation.22 | async-start | bytes 4194304 | tf_op jit(solution)/shard_map/psum | solution.py:190
  941.7 33.9 %copy-start.20 = (bf16[2048,1,128]{2,0,1:T(8,128)(2,1)S(1)}, bf16[2048,1,128]{2,0,1:T(8,128)(2,1)}, u32[]{:S(2)}) copy-start(bf16[2048,1,128]{2,0,1:T(8,128)(2,1)} %copy-done.19) | copy-start | bytes 1572868
  941.7 33.9 %copy-start.22 = (bf16[2048,1,128]{2,0,1:T(8,128)(2,1)S(1)}, bf16[2048,1,128]{2,0,1:T(8,128)(2,1)}, u32[]{:S(2)}) copy-start(bf16[2048,1,128]{2,0,1:T(8,128)(2,1)} %copy-done.21) | copy-start | bytes 1572868
  941.7 33.9 %copy-start.37 = (s32[2048]{0:T(1024)S(1)}, s32[2048]{0:T(1024)}, u32[]{:S(2)}) copy-start(s32[2048]{0:T(1024)} %param.22) | copy-start | bytes 24580
  941.7 33.9 %copy-start.39 = (s32[2048]{0:T(1024)S(1)}, s32[2048]{0:T(1024)}, u32[]{:S(2)}) copy-start(s32[2048]{0:T(1024)} %param.23) | copy-start | bytes 24580
  941.7 33.9 %copy-start.64 = (s32[4]{0:T(128)S(1)}, s32[4]{0:T(128)}, u32[]{:S(2)}) copy-start(s32[4]{0:T(128)} %copy-done.63) | copy-start | bytes 52
  942.9 30.6 %all-to-all-start.4 = ((bf16[512,8,128]{2,0,1:T(8,128)(2,1)}), bf16[512,8,128]{2,0,1:T(8,128)(2,1)S(1)}, u32[]{:S(2)}, u32[]{:S(2)}) async-start(bf16[512,8,128]{2,0,1:T(8,128)(2,1)} %bitcast.301), calls=%async_computation.4 | async-start | bytes 2097152 | tf_op jit(solution)/shard_map/all_to_all | solution.py:207
  992.9 7.9 copy-start.1
  1022.8 7.9 copy-start.1
  1053.0 7.9 copy-start.1
  1083.2 7.9 copy-start.1
  1098.9 17.5 all-to-all-start.6
  1116.4 18.4 all-to-all-start.7
  1134.8 29.6 %all-to-all-start.5 = ((bf16[2048,2,128]{2,1,0:T(2,128)(2,1)}), bf16[2048,2,128]{2,1,0:T(2,128)(2,1)}, u32[]{:S(2)}, u32[]{:S(2)}) async-start(bf16[2048,2,128]{2,1,0:T(2,128)(2,1)} %copy.191), calls=%async_computation.5 | async-start | bytes 2097152 | tf_op jit(solution)/shard_map/all_to_all | solution.py:240
  1139.1 7.9 copy-start.13
  1139.1 7.9 copy-start.29
  1139.1 7.9 copy-start.47
  1139.1 7.9 copy-start.60
  1139.1 147.9 %all-reduce.24.cloned.1.call-start = ((), (), s32[]{:S(2)}) async-start(), calls=%async_computation.24 | async-start | bytes 8388608 | tf_op jit(solution)/shard_map/psum | solution.py:256
  1180.8 353.9 %reduce-scatter.20.cloned.1.call-start = ((), (), s32[]{:S(2)}) async-start(), calls=%async_computation.31 | async-start | bytes 26738688 | tf_op jit(solution)/shard_map/reduce_scatter | solution.py:283
  1196.5 414.3 %reduce-scatter.10.cloned.1.call-start = ((), (), s32[]{:S(2)}) async-start(), calls=%async_computation.26 | async-start | bytes 4456448 | tf_op jit(solution)/shard_map/reduce_scatter | solution.py:267
  1201.7 485.5 %reduce-scatter.12.cloned.1.call-start = ((), (), s32[]{:S(2)}) async-start(), calls=%async_computation.27 | async-start | bytes 4456448 | tf_op jit(solution)/shard_map/reduce_scatter | solution.py:270
  1205.2 589.0 %reduce-scatter.14.cloned.1.call-start = ((), (), s32[]{:S(2)}) async-start(), calls=%async_computation.28 | async-start | bytes 8912896 | tf_op jit(solution)/shard_map/reduce_scatter | solution.py:273
  1214.4 687.4 %reduce-scatter.8.cloned.1.call-start = ((), (), s32[]{:S(2)}) async-start(), calls=%async_computation.25 | async-start | bytes 8912896 | tf_op jit(solution)/shard_map/reduce_scatter | solution.py:264
  1221.6 928.0 %reduce-scatter.16.cloned.1.call-start = ((), (), s32[]{:S(2)}) async-start(), calls=%async_computation.29 | async-start | bytes 26738688 | tf_op jit(solution)/shard_map/reduce_scatter | solution.py:277
  1235.9 1160.8 %reduce-scatter.18.cloned.1.call-start = ((), (), s32[]{:S(2)}) async-start(), calls=%async_computation.30 | async-start | bytes 26738688 | tf_op jit(solution)/shard_map/reduce_scatter | solution.py:280
  1250.2 40.3 %copy-start.54 = (f32[2048]{0:T(1024)S(1)}, f32[2048]{0:T(1024)}, u32[]{:S(2)}) copy-start(f32[2048]{0:T(1024)} %get-tuple-element.389) | copy-start | bytes 24580
  1250.2 110.5 %copy-start.56 = (f32[512]{0:T(512)S(1)}, f32[512]{0:T(512)}, u32[]{:S(2)}) copy-start(f32[512]{0:T(512)} %copy-done.55) | copy-start | bytes 6148
  (36 other events, 100.1 us)
Sparse Core Ops, SparseCore 0:
  10.2 44.3 all-gather.10
  56.8 41.7 all-gather.12
  100.9 47.9 all-gather.8
  182.4 57.7 all-gather.14
  322.4 106.0 all-reduce.17
  430.7 134.3 all-gather.16
  567.4 126.9 all-gather.18
  758.4 108.9 all-reduce.21
  870.3 62.9 all-reduce.19
  1180.9 106.0 all-reduce.23
  1291.1 243.4 reduce-scatter.19
  1538.9 71.8 reduce-scatter.9
  1615.3 71.8 reduce-scatter.11
  1691.7 102.4 reduce-scatter.13
  1798.7 103.0 reduce-scatter.7
  1906.3 243.1 reduce-scatter.15
  2154.1 242.6 reduce-scatter.17
